TPU v7x, 32 devices: a whole 2x2x4 slice. The times are simulated.
32 devices in a mesh: gx: 4 (over z), gy: 4 (over y, x), gz: 2 (over core).
Axes of the slice: x: 2, y: 2, z: 4, core: 2. Of those that a mesh axis runs over, the one named last changes fastest.
Arguments:
- signal: float32 [16, 131072], P(None, ('gx', 'gy', 'gz')), may hold values from -6 to 6
- order: int32 [131072], P(('gx', 'gy', 'gz')), may hold values from 0 to 4095, as said below
- near_tiles: bfloat16 [512, 3, 256, 256], P(('gx', 'gy', 'gz')), may hold values from -0.21875 to 0.21875
- near_list: int32 [512, 3], P(('gx', 'gy', 'gz')), may hold values from 0 to 511, as said below
- leaf_basis: bfloat16 [512, 64, 256], P(('gx', 'gy', 'gz')), may hold values from -0.375 to 0.375
- leaf_transfer: bfloat16 [512, 64, 64], P(('gx', 'gy', 'gz')), may hold values from -0.5 to 0.5
- leaf_coupling: bfloat16 [512, 64, 192], P(('gx', 'gy', 'gz')), may hold values from -0.4375 to 0.4375
- leaf_links: int32 [512, 3], P(('gx', 'gy', 'gz')), may hold values from 0 to 511, as said below
- device_transfer: bfloat16 [32, 64, 64], P(('gx', 'gy', 'gz')), may hold values from -0.5 to 0.5
- device_coupling: bfloat16 [32, 64, 192], P(('gx', 'gy', 'gz')), may hold values from -0.15625 to 0.15625
- device_links: int32 [32, 3], P(('gx', 'gy', 'gz')), may hold values from 0 to 31, as said below
- block_transfer: bfloat16 [16, 64, 64], P(('gx', 'gy')), may hold values from -0.5 to 0.5
- block_coupling: bfloat16 [16, 64, 192], P(('gx', 'gy')), may hold values from -0.15625 to 0.15625
- block_links: int32 [16, 3], P(('gx', 'gy')), may hold values from 0 to 15, as said below
- top_coupling: bfloat16 [4, 64, 192], P('gx'), may hold values from -0.109375 to 0.109375
- top_links: int32 [4, 3], P('gx'), may hold values from 0 to 3, as said below
Outputs:
- smoothed: float32 [16, 131072], P(None, ('gx', 'gy', 'gz'))
- twice: float32 [16, 131072], P(None, ('gx', 'gy', 'gz'))
Inputs may be any that keep to these rules, and one draw needn't show every extreme that they name: `order`: each device's block of 4096 consecutive entries is a permutation of 0 to 4095. `near_list`: row i holds i first, then two different leaves j with 1 <= |j - i| <= 2. `leaf_links`: row i holds three different leaves j with 2 <= |j - i| <= 4. `device_links`: row i holds three different device clusters j with 1 <= |j - i| <= 3. `block_links`: row i holds three different second-level clusters other than i. `top_links`: row i holds three different first-level clusters other than i.
All inputs are finite; a program needn't handle non-finite values.
Results may differ from a plain program's by a relative error of at most 0.0043.
Values may be sent and summed in bfloat16 or wider, within the bound.
No kernel may reach another device: no remote copies, remote signals or barrier semaphores. Data moves between devices by JAX's collectives and lax.ppermute only.
A program may use at most 64 MiB of HBM per device.

v0:
```python
import jax
import jax.numpy as jnp
from jax import lax
from jax.sharding import PartitionSpec as P

NEAR_REACH = 2
LINK_REACH = 4
DEVICE_REACH = 3
HIGH = lax.Precision.HIGHEST


def shifted(block, axis, distance):
    devices = range(lax.axis_size(axis))
    route = [(i - distance, i) for i in devices if i - distance in devices]
    return lax.ppermute(block, axis, route)


def couple(picked, coupling):
    rank_dim = coupling.shape[0]
    link_count = picked.shape[0]
    table = coupling.astype(jnp.float32).reshape(rank_dim, link_count, rank_dim)
    return jnp.einsum("jrk,kjm->rm", picked, table, precision=HIGH)


def spread_down(parent, transfer):
    return jnp.dot(parent, transfer.astype(jnp.float32).T, precision=HIGH)


def relay_side(own_moment, direction):
    window = own_moment[None][:0]
    for step in range(DEVICE_REACH):
        outgoing = jnp.concatenate([own_moment[None], window], axis=0)
        window = shifted(outgoing, ("gx", "gy", "gz"), direction)
    return window


def apply_matrix(
    leaves,
    near_tiles,
    near_list,
    leaf_basis,
    leaf_transfer,
    leaf_coupling,
    leaf_links,
    device_transfer,
    device_coupling,
    device_links,
    block_transfer,
    block_coupling,
    block_links,
    top_coupling,
    top_links,
):
    leaf_dev = leaves.shape[1]
    device = lax.axis_index(("gx", "gy", "gz"))
    first_leaf = device * leaf_dev
    rims = []
    for offset, edge in ((1, leaves[:, leaf_dev - NEAR_REACH :]), (-1, leaves[:, :NEAR_REACH])):
        rims.append(shifted(edge, ("gx", "gy", "gz"), offset))
    widened = jnp.concatenate([rims[0], leaves, rims[1]], axis=1)
    moments = jnp.einsum("rls,lks->rlk", leaves, leaf_basis, preferred_element_type=jnp.float32)
    edges = []
    for offset, edge in ((1, moments[:, leaf_dev - LINK_REACH :]), (-1, moments[:, :LINK_REACH])):
        edges.append(shifted(edge, ("gx", "gy", "gz"), offset))
    wide_moments = jnp.concatenate([edges[0], moments, edges[1]], axis=1)
    transfer_f = leaf_transfer.astype(jnp.float32)
    own_moment = jnp.einsum("rlk,lkm->rm", moments, transfer_f, precision=HIGH)
    block_term = jnp.dot(own_moment, device_transfer[0].astype(jnp.float32), precision=HIGH)
    block_moment = lax.psum(block_term, "gz")
    lower = relay_side(own_moment, 1)
    upper = relay_side(own_moment, -1)
    stacked = jnp.concatenate([lower[::-1], upper], axis=0)
    relative = device_links[0] - device
    position = relative + DEVICE_REACH - (relative > 0).astype(jnp.int32)
    device_picked = stacked[position]
    top_term = jnp.dot(block_moment, block_transfer[0].astype(jnp.float32), precision=HIGH)
    top_moment = lax.psum(top_term, "gy")
    every_top = lax.all_gather(top_moment[None], "gx", axis=0, tiled=True)
    every_block = lax.all_gather(block_moment[None], ("gx", "gy"), axis=0, tiled=True)
    top_field = couple(every_top[top_links[0]], top_coupling[0])
    block_field = couple(every_block[block_links[0]], block_coupling[0]) + spread_down(
        top_field, block_transfer[0]
    )
    device_field = couple(device_picked, device_coupling[0]) + spread_down(
        block_field, device_transfer[0]
    )
    local_links = leaf_links - first_leaf + LINK_REACH
    picked = wide_moments[:, local_links]
    rank_dim = leaf_coupling.shape[1]
    leaf_table = leaf_coupling.astype(jnp.float32).reshape(leaf_dev, rank_dim, -1, rank_dim)
    leaf_field = jnp.einsum("rljk,lkjm->rlm", picked, leaf_table, precision=HIGH)
    leaf_field = leaf_field + jnp.einsum("rm,lkm->rlk", device_field, transfer_f, precision=HIGH)
    far_part = jnp.einsum(
        "rlk,lks->rls",
        leaf_field.astype(jnp.bfloat16),
        leaf_basis,
        preferred_element_type=jnp.float32,
    )
    near_index = near_list - first_leaf + NEAR_REACH
    near_rows = widened[:, near_index]
    near_part = jnp.einsum(
        "rlns,lnst->rlt", near_rows, near_tiles, preferred_element_type=jnp.float32
    )
    return near_part + far_part


def shards(
    signal,
    order,
    near_tiles,
    near_list,
    leaf_basis,
    leaf_transfer,
    leaf_coupling,
    leaf_links,
    device_transfer,
    device_coupling,
    device_links,
    block_transfer,
    block_coupling,
    block_links,
    top_coupling,
    top_links,
):
    matrices = (
        near_tiles,
        near_list,
        leaf_basis,
        leaf_transfer,
        leaf_coupling,
        leaf_links,
        device_transfer,
        device_coupling,
        device_links,
        block_transfer,
        block_coupling,
        block_links,
        top_coupling,
        top_links,
    )
    rhs_count = signal.shape[0]
    leaf_count = near_tiles.shape[0]
    tree = jnp.take(signal, order, axis=1).astype(jnp.bfloat16).reshape(rhs_count, leaf_count, -1)
    first = apply_matrix(tree, *matrices)
    second = apply_matrix(first.astype(jnp.bfloat16), *matrices)
    empty = jnp.zeros_like(signal)
    smoothed = empty.at[:, order].set(first.reshape(rhs_count, -1))
    twice = empty.at[:, order].set(second.reshape(rhs_count, -1))
    return (smoothed, twice)


def solution(mesh):
    in_specs = (
        P(None, ("gx", "gy", "gz")),
        P(("gx", "gy", "gz")),
        P(("gx", "gy", "gz"), None, None, None),
        P(("gx", "gy", "gz"), None),
        P(("gx", "gy", "gz"), None, None),
        P(("gx", "gy", "gz"), None, None),
        P(("gx", "gy", "gz"), None, None),
        P(("gx", "gy", "gz"), None),
        P(("gx", "gy", "gz"), None, None),
        P(("gx", "gy", "gz"), None, None),
        P(("gx", "gy", "gz"), None),
        P(("gx", "gy"), None, None),
        P(("gx", "gy"), None, None),
        P(("gx", "gy"), None),
        P("gx", None, None),
        P("gx", None),
    )
    out_specs = (P(None, ("gx", "gy", "gz")), P(None, ("gx", "gy", "gz")))
    return jax.shard_map(shards, mesh=mesh, in_specs=in_specs, out_specs=out_specs, check_vma=False)
```

profile of v0, /device:TPU:4, one launch (start us, length us, event | category | flops | bytes accessed | tf_op | source)
XLA Modules:
  0.0 253.0 jit_solution(4829175544819906488)
XLA Ops:
  0.6 0.8 compare_and_fusion
  1.4 1.3 broadcast_clamp_fusion
  2.8 1.5 copy.38
  4.4 12.1 %gather_fusion = bf16[4096,16]{1,0:T(8,128)(2,1)S(1)} fusion(bf16[16,4096]{0,1:T(8,128)(2,1)S(1)} %copy.38, s32[4096]{0:T(1024)S(1)} %get-tuple-element.16), kind=kCustom, calls=%fused_computation | custom fusion | bytes 278528 | tf_op jit(solution)/shard_map/jit(_take)/gather | solution.py:143
  16.5 0.3 copy.39
  17.1 0.3 fusion.36
  17.4 2.8 %collective-permute-start.7 = (f32[1,16,64]{2,1,0:T(8,128)S(1)}, f32[1,16,64]{2,1,0:T(8,128)S(1)}, u32[]{:S(2)}, u32[]{:S(2)}) collective-permute-start(f32[1,16,64]{2,1,0:T(8,128)S(1)} %bitcast.193), channel_id=1, source_target_pairs={{1,0},{2,1},{3,2},{4,3},{5,4},{6,5},{7,6},{8,7},{9,8},{10,9},{11,1... | collective-permute-start | bytes 12296 | tf_op jit(solution)/shard_map/ppermute | solution.py:15
  20.2 1.9 collective-permute-start.4
  22.2 2.6 %collective-permute-start = (bf16[16,2,256]{2,0,1:T(8,128)(2,1)S(1)}, bf16[16,2,256]{2,0,1:T(8,128)(2,1)S(1)}, u32[]{:S(2)}, u32[]{:S(2)}) collective-permute-start(bf16[16,2,256]{2,0,1:T(8,128)(2,1)S(1)} %get-tuple-element.14), channel_id=1, source_target_pairs={{0,1},{1,2},{2,3},{3,4},{4,5},{5,6},{6,7},{7,8},{8,9},{9,10},{10,1... | collective-permute-start | bytes 49160 | tf_op jit(solution)/shard_map/ppermute | solution.py:15
  24.8 3.8 %collective-permute-start.1 = (bf16[16,2,256]{2,0,1:T(8,128)(2,1)S(1)}, bf16[16,2,256]{2,0,1:T(8,128)(2,1)S(1)}, u32[]{:S(2)}, u32[]{:S(2)}) collective-permute-start(bf16[16,2,256]{2,0,1:T(8,128)(2,1)S(1)} %get-tuple-element.15), channel_id=1, source_target_pairs={{1,0},{2,1},{3,2},{4,3},{5,4},{6,5},{7,6},{8,7},{9,8},{10,9},{11,1... | collective-permute-start | bytes 49160 | tf_op jit(solution)/shard_map/ppermute | solution.py:15
  28.6 1.9 collective-permute-start.2
  31.3 3.6 %psum.28 = f32[16,64]{1,0:T(8,128)S(1)} all-reduce(f32[16,64]{1,0:T(8,128)S(1)} %fusion.23), channel_id=1, replica_groups=mesh['gx'=4,'gy'=4,'gz'=2] {'gz'}, use_global_device_ids=true, to_apply=%region_0.1 | all-reduce | flops 1024 | bytes 8192 | tf_op jit(solution)/shard_map/psum | solution.py:69
  34.9 35.5 %all-gather = f32[256,64]{1,0:T(8,128)S(1)} all-gather(f32[16,64]{1,0:T(8,128)S(1)} %psum.28), channel_id=2, replica_groups=mesh['gx'=4,'gy'=4,'gz'=2] {'gx','gy'}, dimensions={0}, use_global_device_ids=true | all-gather | bytes 69632 | tf_op jit(solution)/shard_map/all_gather | solution.py:79
  70.6 10.2 %psum.29 = f32[1,16,64]{2,1,0:T(8,128)S(1)} all-reduce(f32[1,16,64]{2,1,0:T(8,128)S(1)} %convolution_bitcast_fusion.11), channel_id=1, replica_groups=mesh['gx'=4,'gy'=4,'gz'=2] {'gy'}, use_global_device_ids=true, to_apply=%region_1.2 | all-reduce | flops 1024 | bytes 8192 | tf_op jit(solution)/shard_map/psum | solution.py:77
  80.8 13.1 %all_gather.13 = f32[4,16,64]{2,1,0:T(8,128)S(1)} all-gather(f32[1,16,64]{2,1,0:T(8,128)S(1)} %psum.29), channel_id=1, replica_groups=mesh['gx'=4,'gy'=4,'gz'=2] {'gx'}, dimensions={0}, use_global_device_ids=true | all-gather | bytes 20480 | tf_op jit(solution)/shard_map/all_gather | solution.py:78
  93.9 0.5 gather_fusion.5
  94.6 0.6 gather_fusion.4
  95.9 1.9 collective-permute-start.5
  97.8 4.5 %collective-permute-start.8 = (f32[2,16,64]{2,1,0:T(8,128)S(1)}, f32[2,16,64]{2,1,0:T(8,128)S(1)}, u32[]{:S(2)}, u32[]{:S(2)}) collective-permute-start(f32[2,16,64]{2,1,0:T(8,128)S(1)} %get-tuple-element.25), channel_id=1, source_target_pairs={{1,0},{2,1},{3,2},{4,3},{5,4},{6,5},{7,6},{8,7},{9,8},{10,9},{11,1... | collective-permute-start | bytes 24584 | tf_op jit(solution)/shard_map/ppermute | solution.py:15
  102.6 0.4 copy.42
  103.0 2.3 collective-permute-start.3
  105.3 2.0 collective-permute-start.6
  107.3 4.4 %collective-permute-start.9 = (f32[3,16,64]{2,1,0:T(8,128)S(1)}, f32[3,16,64]{2,1,0:T(8,128)S(1)}, u32[]{:S(2)}, u32[]{:S(2)}) collective-permute-start(f32[3,16,64]{2,1,0:T(8,128)S(1)} %get-tuple-element.23), channel_id=1, source_target_pairs={{1,0},{2,1},{3,2},{4,3},{5,4},{6,5},{7,6},{8,7},{9,8},{10,9},{11,1... | collective-permute-start | bytes 36872 | tf_op jit(solution)/shard_map/ppermute | solution.py:15
  111.8 0.6 gather_fusion.1
  112.4 3.7 %convolution_bitcast_fusion.1 = f32[16,16,256]{2,1,0:T(8,128)S(1)} fusion(bf16[16,16,3,256]{3,0,2,1:T(8,128)(2,1)S(1)} %bitcast.178, bf16[16,3,256,256]{3,2,1,0:T(8,128)(2,1)} %param.18), kind=kOutput, calls=%fused_computation.17 | convolution fusion | flops 100663296 | bytes 6946816 | tf_op jit(solution)/shard_map/rlns,lnst->rlt/dot_general | solution.py:101
  116.2 0.6 gather_fusion.2
  116.9 0.6 gather_fusion.3
  117.6 0.7 fusion.37
  118.3 0.9 fusion.3
  119.5 0.6 fusion.33
  120.8 1.9 collective-permute-start.17
  122.7 2.4 collective-permute-start.14
  125.1 0.6 fusion.32
  125.8 2.5 psum.30
  128.3 34.8 %all-gather.1 = f32[256,64]{1,0:T(8,128)S(1)} all-gather(f32[16,64]{1,0:T(8,128)S(1)} %psum.30), channel_id=3, replica_groups=mesh['gx'=4,'gy'=4,'gz'=2] {'gx','gy'}, dimensions={0}, use_global_device_ids=true | all-gather | bytes 69632 | tf_op jit(solution)/shard_map/all_gather | solution.py:79
  163.1 1.9 collective-permute-start.10
  165.0 4.5 %collective-permute-start.11 = (bf16[16,2,256]{2,0,1:T(8,128)(2,1)}, bf16[16,2,256]{2,0,1:T(8,128)(2,1)}, u32[]{:S(2)}, u32[]{:S(2)}) collective-permute-start(bf16[16,2,256]{2,0,1:T(8,128)(2,1)} %get-tuple-element.11), channel_id=1, source_target_pairs={{1,0},{2,1},{3,2},{4,3},{5,4},{6,5},{7,6},{8,7},{9,8},{10,9},{11,1... | collective-permute-start | bytes 49160 | tf_op jit(solution)/shard_map/ppermute | solution.py:15
  169.6 10.1 %psum.31 = f32[1,16,64]{2,1,0:T(8,128)S(1)} all-reduce(f32[1,16,64]{2,1,0:T(8,128)S(1)} %convolution_bitcast_fusion.7), channel_id=1, replica_groups=mesh['gx'=4,'gy'=4,'gz'=2] {'gy'}, use_global_device_ids=true, to_apply=%region_4.5 | all-reduce | flops 1024 | bytes 8192 | tf_op jit(solution)/shard_map/psum | solution.py:77
  179.7 13.1 %all_gather.15 = f32[4,16,64]{2,1,0:T(8,128)S(1)} all-gather(f32[1,16,64]{2,1,0:T(8,128)S(1)} %psum.31), channel_id=1, replica_groups=mesh['gx'=4,'gy'=4,'gz'=2] {'gx'}, dimensions={0}, use_global_device_ids=true | all-gather | bytes 20480 | tf_op jit(solution)/shard_map/all_gather | solution.py:78
  192.9 0.5 gather_fusion.10
  193.6 1.9 collective-permute-start.12
  195.5 0.6 gather_fusion.9
  196.4 0.6 pad_maximum_fusion.13
  197.0 1.9 collective-permute-start.15
  198.9 4.5 %collective-permute-start.18 = (f32[2,16,64]{2,1,0:T(8,128)}, f32[2,16,64]{2,1,0:T(8,128)}, u32[]{:S(2)}, u32[]{:S(2)}) collective-permute-start(f32[2,16,64]{2,1,0:T(8,128)} %get-tuple-element.21), channel_id=1, source_target_pairs={{1,0},{2,1},{3,2},{4,3},{5,4},{6,5},{7,6},{8,7},{9,8},{10,9},{11,1... | collective-permute-start | bytes 24584 | tf_op jit(solution)/shard_map/ppermute | solution.py:15
  203.5 0.8 fusion.17
  204.3 2.0 copy.51
  206.2 11.4 %scatter_custom_fusion = f32[16,4096]{0,1:T(8,128)S(1)} fusion(s32[4096]{0:T(1024)} %get-tuple-element.17, f32[4096,16]{1,0:T(8,128)} %copy.51, f32[]{:T(128)} %constant.15.clone.1), kind=kCustom, calls=%fused_computation.42 | custom fusion | bytes 262656 | tf_op jit(solution)/shard_map/scatter | solution.py:147
  217.7 1.3 copy.58
  218.9 2.4 collective-permute-start.13
  221.4 0.7 pad_maximum_fusion.9
  222.1 1.9 collective-permute-start.16
  224.0 4.7 %collective-permute-start.19 = (f32[3,16,64]{2,1,0:T(8,128)S(1)}, f32[3,16,64]{2,1,0:T(8,128)S(1)}, u32[]{:S(2)}, u32[]{:S(2)}) collective-permute-start(f32[3,16,64]{2,1,0:T(8,128)S(1)} %get-tuple-element.19), channel_id=1, source_target_pairs={{1,0},{2,1},{3,2},{4,3},{5,4},{6,5},{7,6},{8,7},{9,8},{10,9},{11,1... | collective-permute-start | bytes 36872 | tf_op jit(solution)/shard_map/ppermute | solution.py:15
  228.8 0.9 pad_maximum_fusion.3
  229.7 0.6 gather_fusion.6
  230.4 3.8 %convolution_bitcast_fusion = f32[16,16,256]{2,1,0:T(8,128)S(1)} fusion(bf16[16,16,3,256]{3,0,2,1:T(8,128)(2,1)S(1)} %bitcast.177, bf16[16,3,256,256]{3,2,1,0:T(8,128)(2,1)} %param.18), kind=kOutput, calls=%fused_computation.15 | convolution fusion | flops 100663296 | bytes 6946816 | tf_op jit(solution)/shard_map/rlns,lnst->rlt/dot_general | solution.py:101
  234.1 0.8 pad_maximum_fusion.1
  234.9 0.6 gather_fusion.7
  235.6 0.7 gather_fusion.8
  236.5 0.7 fusion.39
  237.2 0.9 fusion.4
  238.3 2.0 copy.57
  240.3 11.4 %scatter_custom_fusion.1 = f32[16,4096]{0,1:T(8,128)S(1)} fusion(s32[4096]{0:T(1024)} %get-tuple-element.17, f32[4096,16]{1,0:T(8,128)} %copy.57, f32[]{:T(128)} %constant.15.clone.1), kind=kCustom, calls=%fused_computation.40 | custom fusion | bytes 262656 | tf_op jit(solution)/shard_map/scatter | solution.py:148
  251.7 1.3 copy.59
  (120 shorter events, 4.1 us)
Async XLA Ops:
  0.6 16.3 %copy-start = (bf16[16,64,256]{2,1,0:T(8,128)(2,1)S(1)}, bf16[16,64,256]{2,1,0:T(8,128)(2,1)}, u32[]{:S(2)}) copy-start(bf16[16,64,256]{2,1,0:T(8,128)(2,1)} %param.20) | copy-start | bytes 1572868
  2.8 14.4 %copy-start.1 = (bf16[16,64,64]{2,1,0:T(8,128)(2,1)S(1)}, bf16[16,64,64]{2,1,0:T(8,128)(2,1)}, u32[]{:S(2)}) copy-start(bf16[16,64,64]{2,1,0:T(8,128)(2,1)} %param.21) | copy-start | bytes 393220
  4.2 26.3 %copy-start.23 = (s32[1,3]{1,0:T(1,128)S(1)}, s32[1,3]{1,0:T(1,128)}, u32[]{:S(2)}) copy-start(s32[1,3]{1,0:T(1,128)} %param.26) | copy-start | bytes 40
  4.3 26.3 %copy-start.24 = (s32[1,3]{1,0:T(1,128)S(1)}, s32[1,3]{1,0:T(1,128)}, u32[]{:S(2)}) copy-start(s32[1,3]{1,0:T(1,128)} %param.29) | copy-start | bytes 40
  4.3 26.4 %copy-start.25 = (s32[1,3]{1,0:T(1,128)S(1)}, s32[1,3]{1,0:T(1,128)}, u32[]{:S(2)}) copy-start(s32[1,3]{1,0:T(1,128)} %param.31) | copy-start | bytes 40
  4.3 26.4 %copy-start.21 = (s32[16,3]{0,1:T(4,128)S(1)}, s32[16,3]{0,1:T(4,128)}, u32[]{:S(2)}) copy-start(s32[16,3]{0,1:T(4,128)} %param.23) | copy-start | bytes 580
  4.3 26.4 %copy-start.22 = (s32[16,3]{0,1:T(4,128)S(1)}, s32[16,3]{0,1:T(4,128)}, u32[]{:S(2)}) copy-start(s32[16,3]{0,1:T(4,128)} %param.19) | copy-start | bytes 580
  4.3 26.6 %copy-start.16 = (bf16[1,64,192]{2,1,0:T(8,128)(2,1)S(1)}, bf16[1,64,192]{2,1,0:T(8,128)(2,1)}, u32[]{:S(2)}) copy-start(bf16[1,64,192]{2,1,0:T(8,128)(2,1)} %param.28) | copy-start | bytes 73732
  4.3 26.7 %copy-start.17 = (bf16[1,64,192]{2,1,0:T(8,128)(2,1)S(1)}, bf16[1,64,192]{2,1,0:T(8,128)(2,1)}, u32[]{:S(2)}) copy-start(bf16[1,64,192]{2,1,0:T(8,128)(2,1)} %param.30) | copy-start | bytes 73732
  4.3 26.8 %copy-start.8 = (bf16[1,64,64]{2,1,0:T(8,128)(2,1)S(1)}, bf16[1,64,64]{2,1,0:T(8,128)(2,1)}, u32[]{:S(2)}) copy-start(bf16[1,64,64]{2,1,0:T(8,128)(2,1)} %param.24) | copy-start | bytes 24580
  4.3 66.1 %copy-start.7 = (bf16[1,64,64]{2,1,0:T(8,128)(2,1)S(1)}, bf16[1,64,64]{2,1,0:T(8,128)(2,1)}, u32[]{:S(2)}) copy-start(bf16[1,64,64]{2,1,0:T(8,128)(2,1)} %param.27) | copy-start | bytes 24580
  16.5 85.9 %copy-start.18 = (bf16[1,64,192]{2,1,0:T(8,128)(2,1)S(1)}, bf16[1,64,192]{2,1,0:T(8,128)(2,1)}, u32[]{:S(2)}) copy-start(bf16[1,64,192]{2,1,0:T(8,128)(2,1)} %param.25) | copy-start | bytes 73732
  16.5 86.0 %copy-start.4 = (bf16[16,64,192]{2,1,0:T(8,128)(2,1)S(1)}, bf16[16,64,192]{2,1,0:T(8,128)(2,1)}, u32[]{:S(2)}) copy-start(bf16[16,64,192]{2,1,0:T(8,128)(2,1)} %param.22) | copy-start | bytes 1179652
  17.4 78.5 %collective-permute-start.7 = (f32[1,16,64]{2,1,0:T(8,128)S(1)}, f32[1,16,64]{2,1,0:T(8,128)S(1)}, u32[]{:S(2)}, u32[]{:S(2)}) collective-permute-start(f32[1,16,64]{2,1,0:T(8,128)S(1)} %bitcast.193), channel_id=1, source_target_pairs={{1,0},{2,1},{3,2},{4,3},{5,4},{6,5},{7,6},{8,7},{9,8},{10,9},{11,1... | collective-permute-start | bytes 12296 | tf_op jit(solution)/shard_map/ppermute | solution.py:15
  20.2 75.7 %collective-permute-start.4 = (f32[1,16,64]{2,1,0:T(8,128)S(1)}, f32[1,16,64]{2,1,0:T(8,128)S(1)}, u32[]{:S(2)}, u32[]{:S(2)}) collective-permute-start(f32[1,16,64]{2,1,0:T(8,128)S(1)} %bitcast.194), channel_id=1, source_target_pairs={{0,1},{1,2},{2,3},{3,4},{4,5},{5,6},{6,7},{7,8},{8,9},{9,10},{10,1... | collective-permute-start | bytes 12296 | tf_op jit(solution)/shard_map/ppermute | solution.py:15
  22.2 85.2 %collective-permute-start = (bf16[16,2,256]{2,0,1:T(8,128)(2,1)S(1)}, bf16[16,2,256]{2,0,1:T(8,128)(2,1)S(1)}, u32[]{:S(2)}, u32[]{:S(2)}) collective-permute-start(bf16[16,2,256]{2,0,1:T(8,128)(2,1)S(1)} %get-tuple-element.14), channel_id=1, source_target_pairs={{0,1},{1,2},{2,3},{3,4},{4,5},{5,6},{6,7},{7,8},{8,9},{9,10},{10,1... | collective-permute-start | bytes 49160 | tf_op jit(solution)/shard_map/ppermute | solution.py:15
  24.8 87.0 %collective-permute-start.1 = (bf16[16,2,256]{2,0,1:T(8,128)(2,1)S(1)}, bf16[16,2,256]{2,0,1:T(8,128)(2,1)S(1)}, u32[]{:S(2)}, u32[]{:S(2)}) collective-permute-start(bf16[16,2,256]{2,0,1:T(8,128)(2,1)S(1)} %get-tuple-element.15), channel_id=1, source_target_pairs={{1,0},{2,1},{3,2},{4,3},{5,4},{6,5},{7,6},{8,7},{9,8},{10,9},{11,1... | collective-permute-start | bytes 49160 | tf_op jit(solution)/shard_map/ppermute | solution.py:15
  28.6 87.5 %collective-permute-start.2 = (f32[16,4,64]{2,0,1:T(8,128)S(1)}, f32[16,4,64]{2,0,1:T(8,128)S(1)}, u32[]{:S(2)}, u32[]{:S(2)}) collective-permute-start(f32[16,4,64]{2,0,1:T(8,128)S(1)} %get-tuple-element.12), channel_id=1, source_target_pairs={{0,1},{1,2},{2,3},{3,4},{4,5},{5,6},{6,7},{7,8},{8,9},{9,10},{10,1... | collective-permute-start | bytes 49160 | tf_op jit(solution)/shard_map/ppermute | solution.py:15
  30.7 86.1 %copy-start.20 = (s32[1024]{0:T(1024)}, s32[1024]{0:T(1024)S(1)}, u32[]{:S(2)}) copy-start(s32[1024]{0:T(1024)S(1)} %pad_clamp_fusion.2) | copy-start | bytes 12292
  95.7 20.5 %copy-start.12 = (s32[1024]{0:T(1024)}, s32[1024]{0:T(1024)S(1)}, u32[]{:S(2)}) copy-start(s32[1024]{0:T(1024)S(1)} %pad_clamp_fusion.3) | copy-start | bytes 12292
  95.9 7.0 %collective-permute-start.5 = (f32[2,16,64]{2,1,0:T(8,128)S(1)}, f32[2,16,64]{2,1,0:T(8,128)S(1)}, u32[]{:S(2)}, u32[]{:S(2)}) collective-permute-start(f32[2,16,64]{2,1,0:T(8,128)S(1)} %get-tuple-element.24), channel_id=1, source_target_pairs={{0,1},{1,2},{2,3},{3,4},{4,5},{5,6},{6,7},{7,8},{8,9},{9,10},{10,1... | collective-permute-start | bytes 24584 | tf_op jit(solution)/shard_map/ppermute | solution.py:15
  97.8 7.4 %collective-permute-start.8 = (f32[2,16,64]{2,1,0:T(8,128)S(1)}, f32[2,16,64]{2,1,0:T(8,128)S(1)}, u32[]{:S(2)}, u32[]{:S(2)}) collective-permute-start(f32[2,16,64]{2,1,0:T(8,128)S(1)} %get-tuple-element.25), channel_id=1, source_target_pairs={{1,0},{2,1},{3,2},{4,3},{5,4},{6,5},{7,6},{8,7},{9,8},{10,9},{11,1... | collective-permute-start | bytes 24584 | tf_op jit(solution)/shard_map/ppermute | solution.py:15
  102.4 13.7 %copy-start.14 = (s32[1024]{0:T(1024)}, s32[1024]{0:T(1024)S(1)}, u32[]{:S(2)}) copy-start(s32[1024]{0:T(1024)S(1)} %pad_clamp_fusion.4) | copy-start | bytes 12292
  102.6 14.9 %copy-start.5 = (bf16[1,64,192]{1,2,0:T(8,128)(2,1)}, bf16[1,64,192]{1,2,0:T(8,128)(2,1)S(1)}, u32[]{:S(2)}) copy-start(bf16[1,64,192]{1,2,0:T(8,128)(2,1)S(1)} %copy.44) | copy-start | bytes 73732
  103.0 13.2 %collective-permute-start.3 = (f32[16,4,64]{2,0,1:T(8,128)S(1)}, f32[16,4,64]{2,0,1:T(8,128)S(1)}, u32[]{:S(2)}, u32[]{:S(2)}) collective-permute-start(f32[16,4,64]{2,0,1:T(8,128)S(1)} %get-tuple-element.13), channel_id=1, source_target_pairs={{1,0},{2,1},{3,2},{4,3},{5,4},{6,5},{7,6},{8,7},{9,8},{10,9},{11,1... | collective-permute-start | bytes 49160 | tf_op jit(solution)/shard_map/ppermute | solution.py:15
  105.3 11.5 %collective-permute-start.6 = (f32[3,16,64]{2,1,0:T(8,128)S(1)}, f32[3,16,64]{2,1,0:T(8,128)S(1)}, u32[]{:S(2)}, u32[]{:S(2)}) collective-permute-start(f32[3,16,64]{2,1,0:T(8,128)S(1)} %get-tuple-element.22), channel_id=1, source_target_pairs={{0,1},{1,2},{2,3},{3,4},{4,5},{5,6},{6,7},{7,8},{8,9},{9,10},{10,1... | collective-permute-start | bytes 36872 | tf_op jit(solution)/shard_map/ppermute | solution.py:15
  107.3 9.5 %collective-permute-start.9 = (f32[3,16,64]{2,1,0:T(8,128)S(1)}, f32[3,16,64]{2,1,0:T(8,128)S(1)}, u32[]{:S(2)}, u32[]{:S(2)}) collective-permute-start(f32[3,16,64]{2,1,0:T(8,128)S(1)} %get-tuple-element.23), channel_id=1, source_target_pairs={{1,0},{2,1},{3,2},{4,3},{5,4},{6,5},{7,6},{8,7},{9,8},{10,9},{11,1... | collective-permute-start | bytes 36872 | tf_op jit(solution)/shard_map/ppermute | solution.py:15
  117.6 3.0 %copy-start.9 = (bf16[1,64,64]{2,1,0:T(8,128)(2,1)S(1)}, bf16[1,64,64]{2,1,0:T(8,128)(2,1)}, u32[]{:S(2)}) copy-start(bf16[1,64,64]{2,1,0:T(8,128)(2,1)} %param.24) | copy-start | bytes 24580
  119.5 86.8 %copy-start.3 = (bf16[16,16,256]{2,0,1:T(8,128)(2,1)}, bf16[16,16,256]{2,0,1:T(8,128)(2,1)S(1)}, u32[]{:S(2)}) copy-start(bf16[16,16,256]{2,0,1:T(8,128)(2,1)S(1)} %get-tuple-element.26) | copy-start | bytes 393220
  120.6 83.6 %copy-start.10 = (f32[16,64,1]{1,0,2:T(8,128)}, f32[16,64,1]{1,0,2:T(8,128)S(1)}, u32[]{:S(2)}) copy-start(f32[16,64,1]{1,0,2:T(8,128)S(1)} %fusion.38) | copy-start | bytes 12292
  120.8 75.6 %collective-permute-start.17 = (f32[1,16,64]{2,1,0:T(8,128)S(1)}, f32[1,16,64]{2,1,0:T(8,128)S(1)}, u32[]{:S(2)}, u32[]{:S(2)}) collective-permute-start(f32[1,16,64]{2,1,0:T(8,128)S(1)} %bitcast.197), channel_id=1, source_target_pairs={{1,0},{2,1},{3,2},{4,3},{5,4},{6,5},{7,6},{8,7},{9,8},{10,9},{11,1... | collective-permute-start | bytes 12296 | tf_op jit(solution)/shard_map/ppermute | solution.py:15
  122.7 73.7 %collective-permute-start.14 = (f32[1,16,64]{2,1,0:T(8,128)S(1)}, f32[1,16,64]{2,1,0:T(8,128)S(1)}, u32[]{:S(2)}, u32[]{:S(2)}) collective-permute-start(f32[1,16,64]{2,1,0:T(8,128)S(1)} %bitcast.198), channel_id=1, source_target_pairs={{0,1},{1,2},{2,3},{3,4},{4,5},{5,6},{6,7},{7,8},{8,9},{9,10},{10,1... | collective-permute-start | bytes 12296 | tf_op jit(solution)/shard_map/ppermute | solution.py:15
  163.1 60.9 %collective-permute-start.10 = (bf16[16,2,256]{2,0,1:T(8,128)(2,1)}, bf16[16,2,256]{2,0,1:T(8,128)(2,1)}, u32[]{:S(2)}, u32[]{:S(2)}) collective-permute-start(bf16[16,2,256]{2,0,1:T(8,128)(2,1)} %get-tuple-element.10), channel_id=1, source_target_pairs={{0,1},{1,2},{2,3},{3,4},{4,5},{5,6},{6,7},{7,8},{8,9},{9,10},{10,1... | collective-permute-start | bytes 49160 | tf_op jit(solution)/shard_map/ppermute | solution.py:15
  165.0 63.8 %collective-permute-start.11 = (bf16[16,2,256]{2,0,1:T(8,128)(2,1)}, bf16[16,2,256]{2,0,1:T(8,128)(2,1)}, u32[]{:S(2)}, u32[]{:S(2)}) collective-permute-start(bf16[16,2,256]{2,0,1:T(8,128)(2,1)} %get-tuple-element.11), channel_id=1, source_target_pairs={{1,0},{2,1},{3,2},{4,3},{5,4},{6,5},{7,6},{8,7},{9,8},{10,9},{11,1... | collective-permute-start | bytes 49160 | tf_op jit(solution)/shard_map/ppermute | solution.py:15
  193.6 40.5 %collective-permute-start.12 = (f32[16,4,64]{2,0,1:T(8,128)}, f32[16,4,64]{2,0,1:T(8,128)}, u32[]{:S(2)}, u32[]{:S(2)}) collective-permute-start(f32[16,4,64]{2,0,1:T(8,128)} %get-tuple-element.8), channel_id=1, source_target_pairs={{0,1},{1,2},{2,3},{3,4},{4,5},{5,6},{6,7},{7,8},{8,9},{9,10},{10,1... | collective-permute-start | bytes 49160 | tf_op jit(solution)/shard_map/ppermute | solution.py:15
  197.0 21.9 %collective-permute-start.15 = (f32[2,16,64]{2,1,0:T(8,128)}, f32[2,16,64]{2,1,0:T(8,128)}, u32[]{:S(2)}, u32[]{:S(2)}) collective-permute-start(f32[2,16,64]{2,1,0:T(8,128)} %get-tuple-element.20), channel_id=1, source_target_pairs={{0,1},{1,2},{2,3},{3,4},{4,5},{5,6},{6,7},{7,8},{8,9},{9,10},{10,1... | collective-permute-start | bytes 24584 | tf_op jit(solution)/shard_map/ppermute | solution.py:15
  198.9 22.4 %collective-permute-start.18 = (f32[2,16,64]{2,1,0:T(8,128)}, f32[2,16,64]{2,1,0:T(8,128)}, u32[]{:S(2)}, u32[]{:S(2)}) collective-permute-start(f32[2,16,64]{2,1,0:T(8,128)} %get-tuple-element.21), channel_id=1, source_target_pairs={{1,0},{2,1},{3,2},{4,3},{5,4},{6,5},{7,6},{8,7},{9,8},{10,9},{11,1... | collective-permute-start | bytes 24584 | tf_op jit(solution)/shard_map/ppermute | solution.py:15
  206.2 15.1 %copy-start.11 = (f32[16,64,1]{1,0,2:T(8,128)S(1)}, f32[16,64,1]{1,0,2:T(8,128)}, u32[]{:S(2)}) copy-start(f32[16,64,1]{1,0,2:T(8,128)} %copy-done.10) | copy-start | bytes 12292
  206.2 23.5 %copy-start.15 = (s32[1024]{0:T(1024)S(1)}, s32[1024]{0:T(1024)}, u32[]{:S(2)}) copy-start(s32[1024]{0:T(1024)} %copy-done.14) | copy-start | bytes 12292
  218.9 15.2 %collective-permute-start.13 = (f32[16,4,64]{2,0,1:T(8,128)}, f32[16,4,64]{2,0,1:T(8,128)S(1)}, u32[]{:S(2)}, u32[]{:S(2)}) collective-permute-start(f32[16,4,64]{2,0,1:T(8,128)} %get-tuple-element.9), channel_id=1, source_target_pairs={{1,0},{2,1},{3,2},{4,3},{5,4},{6,5},{7,6},{8,7},{9,8},{10,9},{11,1... | collective-permute-start | bytes 49160 | tf_op jit(solution)/shard_map/ppermute | solution.py:15
  222.1 13.4 %collective-permute-start.16 = (f32[3,16,64]{2,1,0:T(8,128)S(1)}, f32[3,16,64]{2,1,0:T(8,128)S(1)}, u32[]{:S(2)}, u32[]{:S(2)}) collective-permute-start(f32[3,16,64]{2,1,0:T(8,128)S(1)} %get-tuple-element.18), channel_id=1, source_target_pairs={{0,1},{1,2},{2,3},{3,4},{4,5},{5,6},{6,7},{7,8},{8,9},{9,10},{10,1... | collective-permute-start | bytes 36872 | tf_op jit(solution)/shard_map/ppermute | solution.py:15
  224.0 11.5 %collective-permute-start.19 = (f32[3,16,64]{2,1,0:T(8,128)S(1)}, f32[3,16,64]{2,1,0:T(8,128)S(1)}, u32[]{:S(2)}, u32[]{:S(2)}) collective-permute-start(f32[3,16,64]{2,1,0:T(8,128)S(1)} %get-tuple-element.19), channel_id=1, source_target_pairs={{1,0},{2,1},{3,2},{4,3},{5,4},{6,5},{7,6},{8,7},{9,8},{10,9},{11,1... | collective-permute-start | bytes 36872 | tf_op jit(solution)/shard_map/ppermute | solution.py:15
  230.3 4.6 %copy-start.13 = (s32[1024]{0:T(1024)S(1)}, s32[1024]{0:T(1024)}, u32[]{:S(2)}) copy-start(s32[1024]{0:T(1024)} %copy-done.12) | copy-start | bytes 12292
  230.3 5.9 %copy-start.6 = (bf16[1,64,192]{1,2,0:T(8,128)(2,1)S(1)}, bf16[1,64,192]{1,2,0:T(8,128)(2,1)}, u32[]{:S(2)}) copy-start(bf16[1,64,192]{1,2,0:T(8,128)(2,1)} %copy-done.5) | copy-start | bytes 73732
  230.3 5.9 %copy-start.19 = (f32[16,64]{1,0:T(8,128)S(1)}, f32[16,64]{1,0:T(8,128)}, u32[]{:S(2)}) copy-start(f32[16,64]{1,0:T(8,128)} %fusion.17) | copy-start | bytes 12292
  230.4 6.1 %copy-start.2 = (bf16[16,64,64]{2,1,0:T(8,128)(2,1)S(1)}, bf16[16,64,64]{2,1,0:T(8,128)(2,1)}, u32[]{:S(2)}) copy-start(bf16[16,64,64]{2,1,0:T(8,128)(2,1)} %param.21) | copy-start | bytes 393220
where the time goes:
time: 254 us; the launch traced here: 253 us
  blocking collectives  123 us (48%)
  starting transfers between devices  56.5 us (22%)
  local copies, waits for them, and re-layouts  51.6 us (20%)
  matrix products  14.8 us (6%)
  other arithmetic  5.39 us (2%)
    all_gather x2, blocking collectives, apply_matrix(): lax.all_gather(block_moment[None], ('gx', 'gy'), axis=0, tiled=True)  70.3 us
    ppermute x20, starting transfers between devices, shifted(): return lax.ppermute(block, axis, route)  56.5 us
    all_gather x2, blocking collectives, apply_matrix(): every_top = lax.all_gather(top_moment[None], 'gx', axis=0, tiled=True)  26.3 us
    psum x2, blocking collectives, apply_matrix(): top_moment = lax.psum(top_term, 'gy')  20.4 us
    gather x2, local copies, waits for them, and re-layouts, shards(): jnp.take(signal, order, axis=1).astype(jnp.bfloat16)  12.4 us
    scatter x1, local copies, waits for them, and re-layouts, shards(): smoothed = empty.at[:, order].set(first.reshape(rhs_count, -1))  11.4 us
    scatter x1, local copies, waits for them, and re-layouts, shards(): twice = empty.at[:, order].set(second.reshape(rhs_count, -1))  11.4 us
    dot_general x2, matrix products, apply_matrix(): jnp.einsum('rlns,lnst->rlt', near_rows, near_tiles, preferred_element_typ...  7.46 us
  transfers between devices with their start and end apart: 20, of which 0 were waited for; matrix products, arithmetic and copies ran while one was open for 13% of the time, Pallas kernels for 0%

commit v1 on v0

--- a/solution.py
+++ b/solution.py
@@ -74,7 +74,11 @@
     position = relative + DEVICE_REACH - (relative > 0).astype(jnp.int32)
     device_picked = stacked[position]
     top_term = jnp.dot(block_moment, block_transfer[0].astype(jnp.float32), precision=HIGH)
-    top_moment = lax.psum(top_term, "gy")
+    top_moment = top_term
+    for hop in (1, 2):
+        top_moment = top_moment + lax.ppermute(
+            top_moment, "gy", [(dev, dev ^ hop) for dev in range(4)]
+        )
     every_top = lax.all_gather(top_moment[None], "gx", axis=0, tiled=True)
     every_block = lax.all_gather(block_moment[None], ("gx", "gy"), axis=0, tiled=True)
     top_field = couple(every_top[top_links[0]], top_coupling[0])

time: 254 us -> 245 us (0.965)
  blocking collectives: 123 us -> 103 us
  starting transfers between devices: 56.5 us -> 62.8 us
  matrix products: 14.8 us -> 18.9 us
    psum x2 -> x0, blocking collectives: 20.4 us -> none  [apply_matrix(): top_moment = lax.psum(top_term, 'gy')]
    ppermute x0 -> x4, starting transfers between devices: none -> 7.17 us  [apply_matrix(): lax.ppermute(top_moment, 'gy', [(dev, dev ^ hop) for dev in range(4)])]
  transfers between devices with their start and end apart: 20 -> 24, of which waited for: 0 -> 0; matrix products, arithmetic and copies ran while one was open for 13% -> 15% of each run, Pallas kernels for 0% -> 0%
where the time goes in v1:
time: 245 us; the launch traced here: 244 us
  blocking collectives  103 us (42%)
  starting transfers between devices  62.8 us (26%)
  local copies, waits for them, and re-layouts  51.7 us (21%)
  matrix products  18.9 us (8%)
  other arithmetic  5.41 us (2%)
    all_gather x2, blocking collectives, apply_matrix(): lax.all_gather(block_moment[None], ('gx', 'gy'), axis=0, tiled=True)  71.7 us
    ppermute x20, starting transfers between devices, shifted(): return lax.ppermute(block, axis, route)  55.7 us
    all_gather x2, blocking collectives, apply_matrix(): every_top = lax.all_gather(top_moment[None], 'gx', axis=0, tiled=True)  26.3 us
    gather x2, local copies, waits for them, and re-layouts, shards(): jnp.take(signal, order, axis=1).astype(jnp.bfloat16)  12.4 us
    scatter x1, local copies, waits for them, and re-layouts, shards(): smoothed = empty.at[:, order].set(first.reshape(rhs_count, -1))  11.4 us
    scatter x1, local copies, waits for them, and re-layouts, shards(): twice = empty.at[:, order].set(second.reshape(rhs_count, -1))  11.4 us
    dot_general x2, matrix products, apply_matrix(): jnp.einsum('rlns,lnst->rlt', near_rows, near_tiles, preferred_element_typ...  7.46 us
    ppermute x4, starting transfers between devices, apply_matrix(): lax.ppermute(top_moment, 'gy', [(dev, dev ^ hop) for dev in range(4)])  7.17 us
  transfers between devices with their start and end apart: 24, of which 0 were waited for; matrix products, arithmetic and copies ran while one was open for 15% of the time, Pallas kernels for 0%

profile of v1, /device:TPU:4, one launch (start us, length us, event | category | flops | bytes accessed | tf_op | source)
XLA Modules:
  0.0 243.5 jit_solution(1954102983093475536)
XLA Ops:
  0.6 0.8 compare_and_fusion
  1.4 1.3 broadcast_clamp_fusion
  2.8 1.5 copy.24
  4.4 12.1 %gather_fusion = bf16[4096,16]{1,0:T(8,128)(2,1)S(1)} fusion(bf16[16,4096]{0,1:T(8,128)(2,1)S(1)} %copy.24, s32[4096]{0:T(1024)S(1)} %get-tuple-element.14), kind=kCustom, calls=%fused_computation | custom fusion | bytes 278528 | tf_op jit(solution)/shard_map/jit(_take)/gather | solution.py:147
  17.4 2.8 %collective-permute-start.7 = (f32[1,16,64]{2,1,0:T(8,128)S(1)}, f32[1,16,64]{2,1,0:T(8,128)S(1)}, u32[]{:S(2)}, u32[]{:S(2)}) collective-permute-start(f32[1,16,64]{2,1,0:T(8,128)S(1)} %bitcast.191), channel_id=1, source_target_pairs={{1,0},{2,1},{3,2},{4,3},{5,4},{6,5},{7,6},{8,7},{9,8},{10,9},{11,1... | collective-permute-start | bytes 12296 | tf_op jit(solution)/shard_map/ppermute | solution.py:15
  20.2 1.9 collective-permute-start.4
  22.1 2.6 %collective-permute-start = (bf16[16,2,256]{2,0,1:T(8,128)(2,1)S(1)}, bf16[16,2,256]{2,0,1:T(8,128)(2,1)S(1)}, u32[]{:S(2)}, u32[]{:S(2)}) collective-permute-start(bf16[16,2,256]{2,0,1:T(8,128)(2,1)S(1)} %get-tuple-element.12), channel_id=1, source_target_pairs={{0,1},{1,2},{2,3},{3,4},{4,5},{5,6},{6,7},{7,8},{8,9},{9,10},{10,1... | collective-permute-start | bytes 49160 | tf_op jit(solution)/shard_map/ppermute | solution.py:15
  24.8 3.8 %collective-permute-start.1 = (bf16[16,2,256]{2,0,1:T(8,128)(2,1)S(1)}, bf16[16,2,256]{2,0,1:T(8,128)(2,1)S(1)}, u32[]{:S(2)}, u32[]{:S(2)}) collective-permute-start(bf16[16,2,256]{2,0,1:T(8,128)(2,1)S(1)} %get-tuple-element.13), channel_id=1, source_target_pairs={{1,0},{2,1},{3,2},{4,3},{5,4},{6,5},{7,6},{8,7},{9,8},{10,9},{11,1... | collective-permute-start | bytes 49160 | tf_op jit(solution)/shard_map/ppermute | solution.py:15
  28.8 2.5 %psum.14 = f32[16,64]{1,0:T(8,128)S(1)} all-reduce(f32[16,64]{1,0:T(8,128)S(1)} %fusion.25), channel_id=1, replica_groups=mesh['gx'=4,'gy'=4,'gz'=2] {'gz'}, use_global_device_ids=true, to_apply=%region_0.1 | all-reduce | flops 1024 | bytes 8192 | tf_op jit(solution)/shard_map/psum | solution.py:69
  31.4 1.5 collective-permute-start.10
  32.9 37.0 %all-gather = f32[256,64]{1,0:T(8,128)S(1)} all-gather(f32[16,64]{1,0:T(8,128)S(1)} %psum.14), channel_id=2, replica_groups=mesh['gx'=4,'gy'=4,'gz'=2] {'gx','gy'}, dimensions={0}, use_global_device_ids=true | all-gather | bytes 69632 | tf_op jit(solution)/shard_map/all_gather | solution.py:83
  72.0 1.9 collective-permute-start.2
  73.9 3.6 %collective-permute-start.11 = (f32[16,64]{1,0:T(8,128)S(1)}, f32[16,64]{1,0:T(8,128)S(1)}, u32[]{:S(2)}, u32[]{:S(2)}) collective-permute-start(f32[16,64]{1,0:T(8,128)S(1)} %add.143), channel_id=1, source_target_pairs={{0,4},{2,6},{4,0},{6,2},{1,5},{3,7},{5,1},{7,3},{8,12},{10,14},{12... | collective-permute-start | bytes 12296 | tf_op jit(solution)/shard_map/ppermute | solution.py:79
  77.5 1.9 collective-permute-start.5
  79.5 4.5 %collective-permute-start.8 = (f32[2,16,64]{2,1,0:T(8,128)S(1)}, f32[2,16,64]{2,1,0:T(8,128)S(1)}, u32[]{:S(2)}, u32[]{:S(2)}) collective-permute-start(f32[2,16,64]{2,1,0:T(8,128)S(1)} %get-tuple-element.23), channel_id=1, source_target_pairs={{1,0},{2,1},{3,2},{4,3},{5,4},{6,5},{7,6},{8,7},{9,8},{10,9},{11,1... | collective-permute-start | bytes 24584 | tf_op jit(solution)/shard_map/ppermute | solution.py:15
  84.0 13.1 %all-gather.1 = f32[64,64]{1,0:T(8,128)S(1)} all-gather(f32[16,64]{1,0:T(8,128)S(1)} %add.144), channel_id=3, replica_groups=mesh['gx'=4,'gy'=4,'gz'=2] {'gx'}, dimensions={0}, use_global_device_ids=true | all-gather | bytes 20480 | tf_op jit(solution)/shard_map/all_gather | solution.py:82
  98.2 2.0 collective-permute-start.3
  100.2 2.4 collective-permute-start.6
  102.6 4.1 %collective-permute-start.9 = (f32[3,16,64]{2,1,0:T(8,128)S(1)}, f32[3,16,64]{2,1,0:T(8,128)S(1)}, u32[]{:S(2)}, u32[]{:S(2)}) collective-permute-start(f32[3,16,64]{2,1,0:T(8,128)S(1)} %get-tuple-element.21), channel_id=1, source_target_pairs={{1,0},{2,1},{3,2},{4,3},{5,4},{6,5},{7,6},{8,7},{9,8},{10,9},{11,1... | collective-permute-start | bytes 36872 | tf_op jit(solution)/shard_map/ppermute | solution.py:15
  106.7 0.6 gather_fusion.1
  107.3 3.7 %convolution_bitcast_fusion.1 = f32[16,16,256]{2,1,0:T(8,128)S(1)} fusion(bf16[16,16,3,256]{3,0,2,1:T(8,128)(2,1)S(1)} %bitcast.176, bf16[16,3,256,256]{3,2,1,0:T(8,128)(2,1)} %param.18), kind=kOutput, calls=%fused_computation.17 | convolution fusion | flops 100663296 | bytes 6946816 | tf_op jit(solution)/shard_map/rlns,lnst->rlt/dot_general | solution.py:105
  111.1 0.6 gather_fusion.2
  112.5 0.7 fusion.39
  113.2 0.9 fusion.3
  114.3 0.6 fusion.35
  115.2 0.9 fusion.40
  116.1 0.8 fusion.21
  116.9 1.9 collective-permute-start.19
  118.9 2.4 collective-permute-start.16
  121.3 0.6 fusion.34
  121.9 2.5 %psum.15 = f32[16,64]{1,0:T(8,128)S(1)} all-reduce(f32[16,64]{1,0:T(8,128)S(1)} %fusion.21), channel_id=1, replica_groups=mesh['gx'=4,'gy'=4,'gz'=2] {'gz'}, use_global_device_ids=true, to_apply=%region_2.3 | all-reduce | flops 1024 | bytes 8192 | tf_op jit(solution)/shard_map/psum | solution.py:69
  124.4 0.7 fusion.14
  125.1 34.7 %all-gather.2 = f32[256,64]{1,0:T(8,128)S(1)} all-gather(f32[16,64]{1,0:T(8,128)S(1)} %psum.15), channel_id=4, replica_groups=mesh['gx'=4,'gy'=4,'gz'=2] {'gx','gy'}, dimensions={0}, use_global_device_ids=true | all-gather | bytes 69632 | tf_op jit(solution)/shard_map/all_gather | solution.py:83
  159.8 1.9 collective-permute-start.12
  161.7 4.5 %collective-permute-start.13 = (bf16[16,2,256]{2,0,1:T(8,128)(2,1)}, bf16[16,2,256]{2,0,1:T(8,128)(2,1)}, u32[]{:S(2)}, u32[]{:S(2)}) collective-permute-start(bf16[16,2,256]{2,0,1:T(8,128)(2,1)} %get-tuple-element.9), channel_id=1, source_target_pairs={{1,0},{2,1},{3,2},{4,3},{5,4},{6,5},{7,6},{8,7},{9,8},{10,9},{11,1... | collective-permute-start | bytes 49160 | tf_op jit(solution)/shard_map/ppermute | solution.py:15
  166.9 0.8 convolution_bitcast_fusion.7
  167.7 1.9 copy.33
  169.6 11.4 %scatter_custom_fusion = f32[16,4096]{0,1:T(8,128)S(1)} fusion(s32[4096]{0:T(1024)} %get-tuple-element.15, f32[4096,16]{1,0:T(8,128)} %copy.33, f32[]{:T(128)} %constant.15.clone.1), kind=kCustom, calls=%fused_computation.40 | custom fusion | bytes 262656 | tf_op jit(solution)/shard_map/scatter | solution.py:151
  181.1 1.3 copy.36
  182.3 1.9 collective-permute-start.14
  184.3 0.7 add.151
  185.0 2.0 collective-permute-start.23
  187.0 0.7 pad_maximum_fusion.13
  187.7 2.6 %collective-permute-start.17 = (f32[2,16,64]{2,1,0:T(8,128)S(1)}, f32[2,16,64]{2,1,0:T(8,128)S(1)}, u32[]{:S(2)}, u32[]{:S(2)}) collective-permute-start(f32[2,16,64]{2,1,0:T(8,128)S(1)} %get-tuple-element.18), channel_id=1, source_target_pairs={{0,1},{1,2},{2,3},{3,4},{4,5},{5,6},{6,7},{7,8},{8,9},{9,10},{10,1... | collective-permute-start | bytes 24584 | tf_op jit(solution)/shard_map/ppermute | solution.py:15
  190.3 3.8 %collective-permute-start.20 = (f32[2,16,64]{2,1,0:T(8,128)S(1)}, f32[2,16,64]{2,1,0:T(8,128)S(1)}, u32[]{:S(2)}, u32[]{:S(2)}) collective-permute-start(f32[2,16,64]{2,1,0:T(8,128)S(1)} %get-tuple-element.19), channel_id=1, source_target_pairs={{1,0},{2,1},{3,2},{4,3},{5,4},{6,5},{7,6},{8,7},{9,8},{10,9},{11,1... | collective-permute-start | bytes 24584 | tf_op jit(solution)/shard_map/ppermute | solution.py:15
  194.2 13.1 %all-gather.3 = f32[64,64]{1,0:T(8,128)S(1)} all-gather(f32[16,64]{1,0:T(8,128)S(1)} %add.152), channel_id=5, replica_groups=mesh['gx'=4,'gy'=4,'gz'=2] {'gx'}, dimensions={0}, use_global_device_ids=true | all-gather | bytes 20480 | tf_op jit(solution)/shard_map/all_gather | solution.py:82
  207.3 0.7 gather_fusion.10
  208.0 1.0 convolution_bitcast_fusion.6
  209.0 0.8 convolution_add_fusion.2
  209.8 0.9 fusion.19
  210.7 1.9 collective-permute-start.15
  212.6 0.7 pad_maximum_fusion.9
  213.3 2.4 collective-permute-start.18
  215.7 4.2 %collective-permute-start.21 = (f32[3,16,64]{2,1,0:T(8,128)S(1)}, f32[3,16,64]{2,1,0:T(8,128)S(1)}, u32[]{:S(2)}, u32[]{:S(2)}) collective-permute-start(f32[3,16,64]{2,1,0:T(8,128)S(1)} %get-tuple-element.17), channel_id=1, source_target_pairs={{1,0},{2,1},{3,2},{4,3},{5,4},{6,5},{7,6},{8,7},{9,8},{10,9},{11,1... | collective-permute-start | bytes 36872 | tf_op jit(solution)/shard_map/ppermute | solution.py:15
  220.0 0.9 pad_maximum_fusion.3
  221.0 0.7 gather_fusion.6
  221.7 3.8 %convolution_bitcast_fusion = f32[16,16,256]{2,1,0:T(8,128)S(1)} fusion(bf16[16,16,3,256]{3,0,2,1:T(8,128)(2,1)S(1)} %bitcast.175, bf16[16,3,256,256]{3,2,1,0:T(8,128)(2,1)} %param.18), kind=kOutput, calls=%fused_computation.15 | convolution fusion | flops 100663296 | bytes 6946816 | tf_op jit(solution)/shard_map/rlns,lnst->rlt/dot_general | solution.py:105
  225.5 0.6 gather_fusion.7
  226.2 0.7 gather_fusion.8
  227.0 0.7 fusion.41
  227.7 0.9 fusion.4
  228.9 1.9 copy.35
  230.8 11.4 %scatter_custom_fusion.1 = f32[16,4096]{0,1:T(8,128)S(1)} fusion(s32[4096]{0:T(1024)} %get-tuple-element.15, f32[4096,16]{1,0:T(8,128)} %copy.35, f32[]{:T(128)} %constant.15.clone.1), kind=kCustom, calls=%fused_computation.38 | custom fusion | bytes 262656 | tf_op jit(solution)/shard_map/scatter | solution.py:152
  242.3 1.3 copy.37
  (126 shorter events, 6.4 us)
Async XLA Ops:
  0.6 16.3 %copy-start = (bf16[16,64,256]{2,1,0:T(8,128)(2,1)S(1)}, bf16[16,64,256]{2,1,0:T(8,128)(2,1)}, u32[]{:S(2)}) copy-start(bf16[16,64,256]{2,1,0:T(8,128)(2,1)} %param.20) | copy-start | bytes 1572868
  2.8 14.4 %copy-start.1 = (bf16[16,64,64]{2,1,0:T(8,128)(2,1)S(1)}, bf16[16,64,64]{2,1,0:T(8,128)(2,1)}, u32[]{:S(2)}) copy-start(bf16[16,64,64]{2,1,0:T(8,128)(2,1)} %param.21) | copy-start | bytes 393220
  4.2 24.4 %copy-start.9 = (bf16[1,64,64]{2,1,0:T(8,128)(2,1)S(1)}, bf16[1,64,64]{2,1,0:T(8,128)(2,1)}, u32[]{:S(2)}) copy-start(bf16[1,64,64]{2,1,0:T(8,128)(2,1)} %param.24) | copy-start | bytes 24580
  4.3 27.0 %copy-start.8 = (bf16[1,64,64]{2,1,0:T(8,128)(2,1)S(1)}, bf16[1,64,64]{2,1,0:T(8,128)(2,1)}, u32[]{:S(2)}) copy-start(bf16[1,64,64]{2,1,0:T(8,128)(2,1)} %param.27) | copy-start | bytes 24580
  4.3 65.6 %copy-start.21 = (s32[1,3]{1,0:T(1,128)S(1)}, s32[1,3]{1,0:T(1,128)}, u32[]{:S(2)}) copy-start(s32[1,3]{1,0:T(1,128)} %param.26) | copy-start | bytes 40
  4.3 65.6 %copy-start.22 = (s32[1,3]{1,0:T(1,128)S(1)}, s32[1,3]{1,0:T(1,128)}, u32[]{:S(2)}) copy-start(s32[1,3]{1,0:T(1,128)} %param.29) | copy-start | bytes 40
  4.3 65.6 %copy-start.23 = (s32[1,3]{1,0:T(1,128)S(1)}, s32[1,3]{1,0:T(1,128)}, u32[]{:S(2)}) copy-start(s32[1,3]{1,0:T(1,128)} %param.31) | copy-start | bytes 40
  4.3 65.7 %copy-start.19 = (s32[16,3]{0,1:T(4,128)S(1)}, s32[16,3]{0,1:T(4,128)}, u32[]{:S(2)}) copy-start(s32[16,3]{0,1:T(4,128)} %param.23) | copy-start | bytes 580
  4.3 65.7 %copy-start.20 = (s32[16,3]{0,1:T(4,128)S(1)}, s32[16,3]{0,1:T(4,128)}, u32[]{:S(2)}) copy-start(s32[16,3]{0,1:T(4,128)} %param.19) | copy-start | bytes 580
  4.3 66.1 %copy-start.14 = (bf16[1,64,192]{2,1,0:T(8,128)(2,1)S(1)}, bf16[1,64,192]{2,1,0:T(8,128)(2,1)}, u32[]{:S(2)}) copy-start(bf16[1,64,192]{2,1,0:T(8,128)(2,1)} %param.28) | copy-start | bytes 73732
  4.3 66.9 %copy-start.15 = (bf16[1,64,192]{2,1,0:T(8,128)(2,1)S(1)}, bf16[1,64,192]{2,1,0:T(8,128)(2,1)}, u32[]{:S(2)}) copy-start(bf16[1,64,192]{2,1,0:T(8,128)(2,1)} %param.25) | copy-start | bytes 73732
  4.4 67.1 %copy-start.16 = (bf16[1,64,192]{2,1,0:T(8,128)(2,1)S(1)}, bf16[1,64,192]{2,1,0:T(8,128)(2,1)}, u32[]{:S(2)}) copy-start(bf16[1,64,192]{2,1,0:T(8,128)(2,1)} %param.30) | copy-start | bytes 73732
  16.5 55.0 %copy-start.4 = (bf16[16,64,192]{2,1,0:T(8,128)(2,1)S(1)}, bf16[16,64,192]{2,1,0:T(8,128)(2,1)}, u32[]{:S(2)}) copy-start(bf16[16,64,192]{2,1,0:T(8,128)(2,1)} %param.22) | copy-start | bytes 1179652
  17.4 56.5 %collective-permute-start.7 = (f32[1,16,64]{2,1,0:T(8,128)S(1)}, f32[1,16,64]{2,1,0:T(8,128)S(1)}, u32[]{:S(2)}, u32[]{:S(2)}) collective-permute-start(f32[1,16,64]{2,1,0:T(8,128)S(1)} %bitcast.191), channel_id=1, source_target_pairs={{1,0},{2,1},{3,2},{4,3},{5,4},{6,5},{7,6},{8,7},{9,8},{10,9},{11,1... | collective-permute-start | bytes 12296 | tf_op jit(solution)/shard_map/ppermute | solution.py:15
  20.2 57.3 %collective-permute-start.4 = (f32[1,16,64]{2,1,0:T(8,128)S(1)}, f32[1,16,64]{2,1,0:T(8,128)S(1)}, u32[]{:S(2)}, u32[]{:S(2)}) collective-permute-start(f32[1,16,64]{2,1,0:T(8,128)S(1)} %bitcast.192), channel_id=1, source_target_pairs={{0,1},{1,2},{2,3},{3,4},{4,5},{5,6},{6,7},{7,8},{8,9},{9,10},{10,1... | collective-permute-start | bytes 12296 | tf_op jit(solution)/shard_map/ppermute | solution.py:15
  22.1 80.4 %collective-permute-start = (bf16[16,2,256]{2,0,1:T(8,128)(2,1)S(1)}, bf16[16,2,256]{2,0,1:T(8,128)(2,1)S(1)}, u32[]{:S(2)}, u32[]{:S(2)}) collective-permute-start(bf16[16,2,256]{2,0,1:T(8,128)(2,1)S(1)} %get-tuple-element.12), channel_id=1, source_target_pairs={{0,1},{1,2},{2,3},{3,4},{4,5},{5,6},{6,7},{7,8},{8,9},{9,10},{10,1... | collective-permute-start | bytes 49160 | tf_op jit(solution)/shard_map/ppermute | solution.py:15
  24.8 81.8 %collective-permute-start.1 = (bf16[16,2,256]{2,0,1:T(8,128)(2,1)S(1)}, bf16[16,2,256]{2,0,1:T(8,128)(2,1)S(1)}, u32[]{:S(2)}, u32[]{:S(2)}) collective-permute-start(bf16[16,2,256]{2,0,1:T(8,128)(2,1)S(1)} %get-tuple-element.13), channel_id=1, source_target_pairs={{1,0},{2,1},{3,2},{4,3},{5,4},{6,5},{7,6},{8,7},{9,8},{10,9},{11,1... | collective-permute-start | bytes 49160 | tf_op jit(solution)/shard_map/ppermute | solution.py:15
  31.4 40.6 %collective-permute-start.10 = (f32[16,64]{1,0:T(8,128)S(1)}, f32[16,64]{1,0:T(8,128)S(1)}, u32[]{:S(2)}, u32[]{:S(2)}) collective-permute-start(f32[16,64]{1,0:T(8,128)S(1)} %fusion.17), channel_id=1, source_target_pairs={{0,2},{2,0},{4,6},{6,4},{1,3},{3,1},{5,7},{7,5},{8,10},{10,8},{12,... | collective-permute-start | bytes 12296 | tf_op jit(solution)/shard_map/ppermute | solution.py:79
  70.0 41.0 %copy-start.18 = (s32[1024]{0:T(1024)}, s32[1024]{0:T(1024)S(1)}, u32[]{:S(2)}) copy-start(s32[1024]{0:T(1024)S(1)} %pad_clamp_fusion) | copy-start | bytes 12292
  70.0 41.7 %copy-start.17 = (s32[1024]{0:T(1024)}, s32[1024]{0:T(1024)S(1)}, u32[]{:S(2)}) copy-start(s32[1024]{0:T(1024)S(1)} %pad_clamp_fusion.2) | copy-start | bytes 12292
  70.2 40.8 %copy-start.11 = (s32[1024]{0:T(1024)}, s32[1024]{0:T(1024)S(1)}, u32[]{:S(2)}) copy-start(s32[1024]{0:T(1024)S(1)} %pad_clamp_fusion.3) | copy-start | bytes 12292
  71.3 39.7 %copy-start.13 = (s32[1024]{0:T(1024)}, s32[1024]{0:T(1024)S(1)}, u32[]{:S(2)}) copy-start(s32[1024]{0:T(1024)S(1)} %pad_clamp_fusion.4) | copy-start | bytes 12292
  71.4 40.9 %copy-start.6 = (bf16[1,64,192]{1,2,0:T(8,128)(2,1)}, bf16[1,64,192]{1,2,0:T(8,128)(2,1)S(1)}, u32[]{:S(2)}) copy-start(bf16[1,64,192]{1,2,0:T(8,128)(2,1)S(1)} %copy.29) | copy-start | bytes 73732
  71.5 39.4 %copy-start.5 = (bf16[1,64,192]{1,2,0:T(8,128)(2,1)}, bf16[1,64,192]{1,2,0:T(8,128)(2,1)S(1)}, u32[]{:S(2)}) copy-start(bf16[1,64,192]{1,2,0:T(8,128)(2,1)S(1)} %copy.31) | copy-start | bytes 73732
  72.0 39.0 %collective-permute-start.2 = (f32[16,4,64]{2,0,1:T(8,128)S(1)}, f32[16,4,64]{2,0,1:T(8,128)S(1)}, u32[]{:S(2)}, u32[]{:S(2)}) collective-permute-start(f32[16,4,64]{2,0,1:T(8,128)S(1)} %get-tuple-element.10), channel_id=1, source_target_pairs={{0,1},{1,2},{2,3},{3,4},{4,5},{5,6},{6,7},{7,8},{8,9},{9,10},{10,1... | collective-permute-start | bytes 49160 | tf_op jit(solution)/shard_map/ppermute | solution.py:15
  73.9 5.5 %collective-permute-start.11 = (f32[16,64]{1,0:T(8,128)S(1)}, f32[16,64]{1,0:T(8,128)S(1)}, u32[]{:S(2)}, u32[]{:S(2)}) collective-permute-start(f32[16,64]{1,0:T(8,128)S(1)} %add.143), channel_id=1, source_target_pairs={{0,4},{2,6},{4,0},{6,2},{1,5},{3,7},{5,1},{7,3},{8,12},{10,14},{12... | collective-permute-start | bytes 12296 | tf_op jit(solution)/shard_map/ppermute | solution.py:79
  77.5 20.6 %collective-permute-start.5 = (f32[2,16,64]{2,1,0:T(8,128)S(1)}, f32[2,16,64]{2,1,0:T(8,128)S(1)}, u32[]{:S(2)}, u32[]{:S(2)}) collective-permute-start(f32[2,16,64]{2,1,0:T(8,128)S(1)} %get-tuple-element.22), channel_id=1, source_target_pairs={{0,1},{1,2},{2,3},{3,4},{4,5},{5,6},{6,7},{7,8},{8,9},{9,10},{10,1... | collective-permute-start | bytes 24584 | tf_op jit(solution)/shard_map/ppermute | solution.py:15
  79.5 20.7 %collective-permute-start.8 = (f32[2,16,64]{2,1,0:T(8,128)S(1)}, f32[2,16,64]{2,1,0:T(8,128)S(1)}, u32[]{:S(2)}, u32[]{:S(2)}) collective-permute-start(f32[2,16,64]{2,1,0:T(8,128)S(1)} %get-tuple-element.23), channel_id=1, source_target_pairs={{1,0},{2,1},{3,2},{4,3},{5,4},{6,5},{7,6},{8,7},{9,8},{10,9},{11,1... | collective-permute-start | bytes 24584 | tf_op jit(solution)/shard_map/ppermute | solution.py:15
  98.2 12.9 %collective-permute-start.3 = (f32[16,4,64]{2,0,1:T(8,128)S(1)}, f32[16,4,64]{2,0,1:T(8,128)S(1)}, u32[]{:S(2)}, u32[]{:S(2)}) collective-permute-start(f32[16,4,64]{2,0,1:T(8,128)S(1)} %get-tuple-element.11), channel_id=1, source_target_pairs={{1,0},{2,1},{3,2},{4,3},{5,4},{6,5},{7,6},{8,7},{9,8},{10,9},{11,1... | collective-permute-start | bytes 49160 | tf_op jit(solution)/shard_map/ppermute | solution.py:15
  100.2 11.5 %collective-permute-start.6 = (f32[3,16,64]{2,1,0:T(8,128)S(1)}, f32[3,16,64]{2,1,0:T(8,128)S(1)}, u32[]{:S(2)}, u32[]{:S(2)}) collective-permute-start(f32[3,16,64]{2,1,0:T(8,128)S(1)} %get-tuple-element.20), channel_id=1, source_target_pairs={{0,1},{1,2},{2,3},{3,4},{4,5},{5,6},{6,7},{7,8},{8,9},{9,10},{10,1... | collective-permute-start | bytes 36872 | tf_op jit(solution)/shard_map/ppermute | solution.py:15
  102.6 9.1 %collective-permute-start.9 = (f32[3,16,64]{2,1,0:T(8,128)S(1)}, f32[3,16,64]{2,1,0:T(8,128)S(1)}, u32[]{:S(2)}, u32[]{:S(2)}) collective-permute-start(f32[3,16,64]{2,1,0:T(8,128)S(1)} %get-tuple-element.21), channel_id=1, source_target_pairs={{1,0},{2,1},{3,2},{4,3},{5,4},{6,5},{7,6},{8,7},{9,8},{10,9},{11,1... | collective-permute-start | bytes 36872 | tf_op jit(solution)/shard_map/ppermute | solution.py:15
  112.5 3.6 %copy-start.10 = (bf16[1,64,64]{2,1,0:T(8,128)(2,1)S(1)}, bf16[1,64,64]{2,1,0:T(8,128)(2,1)}, u32[]{:S(2)}) copy-start(bf16[1,64,64]{2,1,0:T(8,128)(2,1)} %param.24) | copy-start | bytes 24580
  114.3 55.3 %copy-start.3 = (bf16[16,16,256]{2,0,1:T(8,128)(2,1)}, bf16[16,16,256]{2,0,1:T(8,128)(2,1)S(1)}, u32[]{:S(2)}) copy-start(bf16[16,16,256]{2,0,1:T(8,128)(2,1)S(1)} %get-tuple-element.24) | copy-start | bytes 393220
  116.9 68.1 %collective-permute-start.19 = (f32[1,16,64]{2,1,0:T(8,128)}, f32[1,16,64]{2,1,0:T(8,128)}, u32[]{:S(2)}, u32[]{:S(2)}) collective-permute-start(f32[1,16,64]{2,1,0:T(8,128)} %bitcast.45), channel_id=1, source_target_pairs={{1,0},{2,1},{3,2},{4,3},{5,4},{6,5},{7,6},{8,7},{9,8},{10,9},{11,1... | collective-permute-start | bytes 12296 | tf_op jit(solution)/shard_map/ppermute | solution.py:15
  118.9 68.1 %collective-permute-start.16 = (f32[1,16,64]{2,1,0:T(8,128)}, f32[1,16,64]{2,1,0:T(8,128)}, u32[]{:S(2)}, u32[]{:S(2)}) collective-permute-start(f32[1,16,64]{2,1,0:T(8,128)} %bitcast.45), channel_id=1, source_target_pairs={{0,1},{1,2},{2,3},{3,4},{4,5},{5,6},{6,7},{7,8},{8,9},{9,10},{10,1... | collective-permute-start | bytes 12296 | tf_op jit(solution)/shard_map/ppermute | solution.py:15
  159.8 55.9 %collective-permute-start.12 = (bf16[16,2,256]{2,0,1:T(8,128)(2,1)}, bf16[16,2,256]{2,0,1:T(8,128)(2,1)}, u32[]{:S(2)}, u32[]{:S(2)}) collective-permute-start(bf16[16,2,256]{2,0,1:T(8,128)(2,1)} %get-tuple-element.8), channel_id=1, source_target_pairs={{0,1},{1,2},{2,3},{3,4},{4,5},{5,6},{6,7},{7,8},{8,9},{9,10},{10,1... | collective-permute-start | bytes 49160 | tf_op jit(solution)/shard_map/ppermute | solution.py:15
  161.7 58.3 %collective-permute-start.13 = (bf16[16,2,256]{2,0,1:T(8,128)(2,1)}, bf16[16,2,256]{2,0,1:T(8,128)(2,1)}, u32[]{:S(2)}, u32[]{:S(2)}) collective-permute-start(bf16[16,2,256]{2,0,1:T(8,128)(2,1)} %get-tuple-element.9), channel_id=1, source_target_pairs={{1,0},{2,1},{3,2},{4,3},{5,4},{6,5},{7,6},{8,7},{9,8},{10,9},{11,1... | collective-permute-start | bytes 49160 | tf_op jit(solution)/shard_map/ppermute | solution.py:15
  166.3 16.1 %collective-permute-start.22 = (f32[16,64]{1,0:T(8,128)}, f32[16,64]{1,0:T(8,128)}, u32[]{:S(2)}, u32[]{:S(2)}) collective-permute-start(f32[16,64]{1,0:T(8,128)} %fusion.14), channel_id=1, source_target_pairs={{0,2},{2,0},{4,6},{6,4},{1,3},{3,1},{5,7},{7,5},{8,10},{10,8},{12,... | collective-permute-start | bytes 12296 | tf_op jit(solution)/shard_map/ppermute | solution.py:79
  182.3 43.1 %collective-permute-start.14 = (f32[16,4,64]{2,0,1:T(8,128)}, f32[16,4,64]{2,0,1:T(8,128)S(1)}, u32[]{:S(2)}, u32[]{:S(2)}) collective-permute-start(f32[16,4,64]{2,0,1:T(8,128)} %get-tuple-element.6), channel_id=1, source_target_pairs={{0,1},{1,2},{2,3},{3,4},{4,5},{5,6},{6,7},{7,8},{8,9},{9,10},{10,1... | collective-permute-start | bytes 49160 | tf_op jit(solution)/shard_map/ppermute | solution.py:15
  185.0 5.3 %collective-permute-start.23 = (f32[16,64]{1,0:T(8,128)S(1)}, f32[16,64]{1,0:T(8,128)S(1)}, u32[]{:S(2)}, u32[]{:S(2)}) collective-permute-start(f32[16,64]{1,0:T(8,128)S(1)} %add.151), channel_id=1, source_target_pairs={{0,4},{2,6},{4,0},{6,2},{1,5},{3,7},{5,1},{7,3},{8,12},{10,14},{12... | collective-permute-start | bytes 12296 | tf_op jit(solution)/shard_map/ppermute | solution.py:79
  187.7 23.0 %collective-permute-start.17 = (f32[2,16,64]{2,1,0:T(8,128)S(1)}, f32[2,16,64]{2,1,0:T(8,128)S(1)}, u32[]{:S(2)}, u32[]{:S(2)}) collective-permute-start(f32[2,16,64]{2,1,0:T(8,128)S(1)} %get-tuple-element.18), channel_id=1, source_target_pairs={{0,1},{1,2},{2,3},{3,4},{4,5},{5,6},{6,7},{7,8},{8,9},{9,10},{10,1... | collective-permute-start | bytes 24584 | tf_op jit(solution)/shard_map/ppermute | solution.py:15
  190.3 22.3 %collective-permute-start.20 = (f32[2,16,64]{2,1,0:T(8,128)S(1)}, f32[2,16,64]{2,1,0:T(8,128)S(1)}, u32[]{:S(2)}, u32[]{:S(2)}) collective-permute-start(f32[2,16,64]{2,1,0:T(8,128)S(1)} %get-tuple-element.19), channel_id=1, source_target_pairs={{1,0},{2,1},{3,2},{4,3},{5,4},{6,5},{7,6},{8,7},{9,8},{10,9},{11,1... | collective-permute-start | bytes 24584 | tf_op jit(solution)/shard_map/ppermute | solution.py:15
  210.7 14.8 %collective-permute-start.15 = (f32[16,4,64]{2,0,1:T(8,128)}, f32[16,4,64]{2,0,1:T(8,128)S(1)}, u32[]{:S(2)}, u32[]{:S(2)}) collective-permute-start(f32[16,4,64]{2,0,1:T(8,128)} %get-tuple-element.7), channel_id=1, source_target_pairs={{1,0},{2,1},{3,2},{4,3},{5,4},{6,5},{7,6},{8,7},{9,8},{10,9},{11,1... | collective-permute-start | bytes 49160 | tf_op jit(solution)/shard_map/ppermute | solution.py:15
  213.3 12.8 %collective-permute-start.18 = (f32[3,16,64]{2,1,0:T(8,128)S(1)}, f32[3,16,64]{2,1,0:T(8,128)S(1)}, u32[]{:S(2)}, u32[]{:S(2)}) collective-permute-start(f32[3,16,64]{2,1,0:T(8,128)S(1)} %get-tuple-element.16), channel_id=1, source_target_pairs={{0,1},{1,2},{2,3},{3,4},{4,5},{5,6},{6,7},{7,8},{8,9},{9,10},{10,1... | collective-permute-start | bytes 36872 | tf_op jit(solution)/shard_map/ppermute | solution.py:15
  215.7 10.4 %collective-permute-start.21 = (f32[3,16,64]{2,1,0:T(8,128)S(1)}, f32[3,16,64]{2,1,0:T(8,128)S(1)}, u32[]{:S(2)}, u32[]{:S(2)}) collective-permute-start(f32[3,16,64]{2,1,0:T(8,128)S(1)} %get-tuple-element.17), channel_id=1, source_target_pairs={{1,0},{2,1},{3,2},{4,3},{5,4},{6,5},{7,6},{8,7},{9,8},{10,9},{11,1... | collective-permute-start | bytes 36872 | tf_op jit(solution)/shard_map/ppermute | solution.py:15
  221.7 3.8 %copy-start.12 = (s32[1024]{0:T(1024)S(1)}, s32[1024]{0:T(1024)}, u32[]{:S(2)}) copy-start(s32[1024]{0:T(1024)} %copy-done.11) | copy-start | bytes 12292
  221.7 5.2 %copy-start.7 = (bf16[1,64,192]{1,2,0:T(8,128)(2,1)S(1)}, bf16[1,64,192]{1,2,0:T(8,128)(2,1)}, u32[]{:S(2)}) copy-start(bf16[1,64,192]{1,2,0:T(8,128)(2,1)} %copy-done.6) | copy-start | bytes 73732
  221.7 5.3 %copy-start.2 = (bf16[16,64,64]{2,1,0:T(8,128)(2,1)S(1)}, bf16[16,64,64]{2,1,0:T(8,128)(2,1)}, u32[]{:S(2)}) copy-start(bf16[16,64,64]{2,1,0:T(8,128)(2,1)} %param.21) | copy-start | bytes 393220
